TPU v7x, 256 devices: a whole 4x4x8 slice. The times are simulated.
256 devices in a mesh: gx: 4 (over z_lo), gy: 8 (over x, z_hi), gz: 8 (over y, core).
Axes of the slice: x: 4, y: 4, z: 8 (z_hi: 2, z_lo: 4; z = z_hi * 4 + z_lo), core: 2. Of those that a mesh axis runs over, the one named last changes fastest.
Arguments:
- attn_out: bfloat16 [16384, 8192], P('gx', ('gy', 'gz')), may hold values from -16 to 16
- out_grad: bfloat16 [16384, 8192], P('gx', ('gz', 'gy')), may hold values from -0.046875 to 0.046875
- valid_counts: int32 [16], P('gx'), may hold values from 128 to 1024
Outputs:
- weight_grad: float32 [8192, 8192], P(('gy', 'gx'), 'gz')
Inputs may be any that keep to these rules, and one draw needn't show every extreme that they name: `valid_counts`: valid tokens of a packed row come first, padding after.
All inputs are finite; a program needn't handle non-finite values.
Results may differ from a plain program's by a relative error of at most 0.0003.
Values may be sent and summed in bfloat16 or wider, within the bound.
A program may use at most 64 MiB of HBM per device.

v0:
```python
import jax
import jax.numpy as jnp
from jax import lax
from jax.sharding import Mesh
from jax.sharding import PartitionSpec as P

GY = ("gy_0", "gy_1")
GY_GZ = ("gy_0", "gy_1", "gz")
GZ_GY = ("gz", "gy_0", "gy_1")
GY_GX = ("gy_0", "gy_1", "gx")


def whole_of(value, axes, dim):
    out = value
    for number in range(len(axes) - 1, -1, -1):
        out = lax.all_gather(out, axes[number], axis=dim, tiled=True)
    return out


def split_up(value, dim, peers):
    lengths = value.shape
    tiles = value.reshape(*lengths[:dim], peers, lengths[dim] // peers, *lengths[dim + 1 :])
    return jnp.moveaxis(tiles, dim, 0)


def summed_on_arrival(value, axis, dim):
    tiles = split_up(value, dim, lax.axis_size(axis))
    arrived = lax.all_to_all(tiles, axis, split_axis=0, concat_axis=0, tiled=True)
    return arrived.sum(axis=0)


def transpose_product(inputs, grads):
    return lax.dot_general(
        inputs, grads, (((0,), (0,)), ((), ())), preferred_element_type=jnp.float32
    )


def shards(attn_out, out_grad, valid_counts):
    rows_here = valid_counts.shape[0]
    slot_count = attn_out.shape[0] // rows_here
    positions = lax.broadcasted_iota(jnp.int32, (rows_here, slot_count), 1)
    kept_rows = (positions < valid_counts[:, None]).reshape(-1)
    gathered_inputs = lax.all_gather(attn_out, "gz", axis=1, tiled=True)
    gathered_grads = whole_of(out_grad, GY, 1)
    masked = jnp.where(kept_rows[:, None], gathered_grads, jnp.zeros((), gathered_grads.dtype))
    partial_grad = transpose_product(gathered_inputs, masked)
    return summed_on_arrival(partial_grad, "gx", 0)


def solution(mesh):
    split = Mesh(
        mesh.devices.reshape(mesh.shape["gx"], 4, 2, mesh.shape["gz"]), ("gx", "gy_0", "gy_1", "gz")
    )
    return jax.shard_map(
        shards,
        mesh=split,
        in_specs=(P("gx", GY_GZ), P("gx", GZ_GY), P("gx")),
        out_specs=P(GY_GX, "gz"),
        check_vma=False,
    )
```

profile of v0, /device:TPU:8, one launch (start us, length us, event | category | flops | bytes accessed | tf_op | source)
XLA Modules:
  0.0 345.3 jit_solution(17290514149555261762)
XLA Ops:
  6.5 0.0 all-gather.4.cloned.1.call-start
  6.5 0.7 all-gather.4.cloned.1.call-update
  7.3 0.0 all-gather.8.cloned.1.call-start
  7.3 0.7 all-gather.8.cloned.1.call-update
  8.0 0.0 all-gather.6.cloned.1.call-start
  8.1 69.1 %all-gather.4.cloned.1.call-done = bf16[4096,256]{1,0:T(8,128)(2,1)} async-done(((bf16[4096,128]{1,0:T(8,128)(2,1)}), bf16[4096,256]{1,0:T(8,128)(2,1)}) %all-gather.4.cloned.1.call-update) | async-done | bytes 2097168 | tf_op jit(solution)/shard_map/all_gather | solution.py:16
  77.1 0.0 all-gather.6.cloned.1.call-update
  77.2 0.7 fusion.4
  77.9 53.2 %all-gather.8.cloned.1.call-done = bf16[4096,1024]{1,0:T(8,128)(2,1)} async-done(((bf16[4096,128]{1,0:T(8,128)(2,1)}), bf16[4096,1024]{1,0:T(8,128)(2,1)}) %all-gather.8.cloned.1.call-update) | async-done | bytes 8388624 | tf_op jit(solution)/shard_map/all_gather | solution.py:43
  131.1 92.2 %all-gather.6.cloned.1.call-done = bf16[4096,1024]{1,0:T(8,128)(2,1)} async-done(((bf16[4096,256]{1,0:T(8,128)(2,1)}), bf16[4096,1024]{1,0:T(8,128)(2,1)}) %all-gather.6.cloned.1.call-update) | async-done | bytes 8388624 | tf_op jit(solution)/shard_map/all_gather | solution.py:16
  223.3 15.3 %fusion = f32[1024,1024]{0,1:T(8,128)S(1)} fusion(bf16[4096,1024]{1,0:T(8,128)(2,1)} %all-gather.8.cloned.1.call-done, bf16[4096,1024]{1,0:T(8,128)(2,1)} %all-gather.6.cloned.1.call-done, pred[4096]{0:T(1024)(128)(4,1)S(1)} %bitcast.10), kind=kOutput, calls=%fused_computation | convolution fusion | flops 8594128896 | bytes 20975616 | tf_op jit(solution)/shard_map/dot_general | solution.py:33
  238.6 96.5 %all_to_all.5 = f32[4,256,1024]{2,1,0:T(8,128)} all-to-all(f32[4,256,1024]{2,1,0:T(8,128)S(1)} %bitcast.9), channel_id=1, replica_groups=mesh['gx'=4,'gy_0'=4,'gy_1'=2,'gz'=8] {'gx'}, dimensions={0} | all-to-all | bytes 8388608 | tf_op jit(solution)/shard_map/all_to_all | solution.py:28
  335.1 3.7 %reduce_sum.9 = f32[256,1024]{1,0:T(8,128)} reduce(f32[4,256,1024]{2,1,0:T(8,128)} %all_to_all.5, f32[]{:T(128)} %constant.1.clone.1), dimensions={0}, to_apply=%region_0.1 | reduce | flops 786432 | bytes 5242884 | tf_op jit(solution)/shard_map/reduce_sum | solution.py:29
  (1 shorter events, 0.0 us)
Async XLA Ops:
  6.5 70.6 %all-gather.4.cloned.1.call-start = ((), (), s32[]{:S(2)}) async-start(), calls=%async_computation.1 | async-start | bytes 3145728 | tf_op jit(solution)/shard_map/all_gather | solution.py:16
  7.3 123.8 %all-gather.8.cloned.1.call-start = ((), (), s32[]{:S(2)}) async-start(), calls=%async_computation.3 | async-start | bytes 9437184 | tf_op jit(solution)/shard_map/all_gather | solution.py:43
  8.0 215.3 %all-gather.6.cloned.1.call-start = ((), (), s32[]{:S(2)}) async-start(), calls=%async_computation.2 | async-start | bytes 10485760 | tf_op jit(solution)/shard_map/all_gather | solution.py:16
Sparse Core Ops, SparseCore 0:
  9.1 67.9 all-gather.3
  79.0 52.0 all-gather.7
  132.9 90.3 all-gather.5
where the time goes:
time: 345 us
  waiting for transfers between devices  216 us (63%)
  blocking collectives  96.5 us (28%)
  matrix products  15.3 us (4%)
  between operations  13.1 us (4%)
  other arithmetic  4.42 us (1%)
    all_gather x2, waiting for transfers between devices, whole_of(): out = lax.all_gather(out, axes[number], axis=dim, tiled=True)  161 us
    all_to_all x1, blocking collectives, summed_on_arrival(): lax.all_to_all(tiles, axis, split_axis=0, concat_axis=0, tiled=True)  96.5 us
    all_gather x1, waiting for transfers between devices, shards(): gathered_inputs = lax.all_gather(attn_out, 'gz', axis=1, tiled=True)  53.2 us
    dot_general x1, matrix products, transpose_product(): lax.dot_general(inputs, grads, (((0,), (0,)), ((), ())), preferred_elemen...  15.3 us
  transfers between devices with their start and end apart: 3, of which 3 were waited for; matrix products, arithmetic and copies ran while one was open for 0% of the time, Pallas kernels for 0%

commit v1 on v0

--- a/solution.py
+++ b/solution.py
@@ -40,7 +40,14 @@
     slot_count = attn_out.shape[0] // rows_here
     positions = lax.broadcasted_iota(jnp.int32, (rows_here, slot_count), 1)
     kept_rows = (positions < valid_counts[:, None]).reshape(-1)
-    gathered_inputs = lax.all_gather(attn_out, "gz", axis=1, tiled=True)
+    ways = lax.axis_size("gz")
+    pieces = [attn_out]
+    for far in range(1, ways):
+        pieces.append(
+            lax.ppermute(pieces[far - 1], "gz", [(d, (d - 1) % ways) for d in range(ways)])
+        )
+    line = jnp.concatenate(pieces, axis=1)
+    gathered_inputs = jnp.roll(line, lax.axis_index("gz") * attn_out.shape[1], axis=1)
     gathered_grads = whole_of(out_grad, GY, 1)
     masked = jnp.where(kept_rows[:, None], gathered_grads, jnp.zeros((), gathered_grads.dtype))
     partial_grad = transpose_product(gathered_inputs, masked)

time: 345 us -> 316 us (0.916)
  waiting for transfers between devices: 216 us -> 144 us
  local copies, waits for them, and re-layouts: 0.01 us -> 26.4 us
  starting transfers between devices: 0.08 us -> 12.8 us
    all_gather x2, waiting for transfers between devices: 161 us -> 69.8 us  [whole_of(): out = lax.all_gather(out, axes[number], axis=dim, tiled=True)]
    ppermute x0 -> x7, waiting for transfers between devices: none -> 73.5 us  [shards(): lax.ppermute(pieces[far - 1], 'gz', [(d, (d - 1) % ways) for d in range(w...]
    all_gather x1 -> x0, waiting for transfers between devices: 53.2 us -> none  [shards(): gathered_inputs = lax.all_gather(attn_out, 'gz', axis=1, tiled=True)]
    unnamed x1 -> x22, local copies, waits for them, and re-layouts: 0.01 us -> 25.3 us
    ppermute x0 -> x7, starting transfers between devices: none -> 12.7 us  [shards(): lax.ppermute(pieces[far - 1], 'gz', [(d, (d - 1) % ways) for d in range(w...]
  transfers between devices with their start and end apart: 3 -> 9, of which waited for: 3 -> 8; matrix products, arithmetic and copies ran while one was open for 0% -> 8% of each run, Pallas kernels for 0% -> 0%
where the time goes in v1:
time: 316 us; the launch traced here: 314 us
  waiting for transfers between devices  144 us (46%)
  blocking collectives  97.2 us (31%)
  local copies, waits for them, and re-layouts  26.4 us (8%)
  matrix products  15.3 us (5%)
  between operations  13.4 us (4%)
  starting transfers between devices  12.8 us (4%)
  other arithmetic  4.42 us (1%)
    all_to_all x1, blocking collectives, summed_on_arrival(): lax.all_to_all(tiles, axis, split_axis=0, concat_axis=0, tiled=True)  97.2 us
    ppermute x7, waiting for transfers between devices, shards(): lax.ppermute(pieces[far - 1], 'gz', [(d, (d - 1) % ways) for d in range(w...  73.5 us
    all_gather x2, waiting for transfers between devices, whole_of(): out = lax.all_gather(out, axes[number], axis=dim, tiled=True)  69.8 us
    unnamed x22, local copies, waits for them, and re-layouts  25.3 us
    dot_general x1, matrix products, transpose_product(): lax.dot_general(inputs, grads, (((0,), (0,)), ((), ())), preferred_elemen...  15.3 us
    ppermute x7, starting transfers between devices, shards(): lax.ppermute(pieces[far - 1], 'gz', [(d, (d - 1) % ways) for d in range(w...  12.7 us
  transfers between devices with their start and end apart: 9, of which 8 were waited for; matrix products, arithmetic and copies ran while one was open for 8% of the time, Pallas kernels for 0%

profile of v1, /device:TPU:8, one launch (start us, length us, event | category | flops | bytes accessed | tf_op | source)
XLA Modules:
  0.0 313.6 jit_solution(11945423491475501619)
XLA Ops:
  7.3 69.8 %all-gather.3.cloned.1.call-done = bf16[4096,256]{1,0:T(8,128)(2,1)} async-done(((bf16[4096,128]{1,0:T(8,128)(2,1)}), bf16[4096,256]{1,0:T(8,128)(2,1)}) %all-gather.3.cloned.1.call-update) | async-done | bytes 2097168 | tf_op jit(solution)/shard_map/all_gather | solution.py:16
  77.2 12.6 %collective-permute-done = bf16[4096,128]{1,0:T(8,128)(2,1)S(1)} collective-permute-done((bf16[4096,128]{1,0:T(8,128)(2,1)}, bf16[4096,128]{1,0:T(8,128)(2,1)S(1)}, u32[]{:S(2)}, u32[]{:S(2)}) %collective-permute-start) | collective-permute-done | bytes 1048608 | tf_op jit(solution)/shard_map/ppermute | solution.py:47
  89.8 1.8 collective-permute-start.1
  91.6 12.3 %collective-permute-done.1 = bf16[4096,128]{1,0:T(8,128)(2,1)S(1)} collective-permute-done((bf16[4096,128]{1,0:T(8,128)(2,1)S(1)}, bf16[4096,128]{1,0:T(8,128)(2,1)S(1)}, u32[]{:S(2)}, u32[]{:S(2)}) %collective-permute-start.1) | collective-permute-done | bytes 1048608 | tf_op jit(solution)/shard_map/ppermute | solution.py:47
  103.9 2.3 collective-permute-start.2
  106.3 12.3 %collective-permute-done.2 = bf16[4096,128]{1,0:T(8,128)(2,1)S(1)} collective-permute-done((bf16[4096,128]{1,0:T(8,128)(2,1)S(1)}, bf16[4096,128]{1,0:T(8,128)(2,1)S(1)}, u32[]{:S(2)}, u32[]{:S(2)}) %collective-permute-start.2) | collective-permute-done | bytes 1048608 | tf_op jit(solution)/shard_map/ppermute | solution.py:47
  119.5 2.3 collective-permute-start.3
  121.9 12.3 %collective-permute-done.3 = bf16[4096,128]{1,0:T(8,128)(2,1)} collective-permute-done((bf16[4096,128]{1,0:T(8,128)(2,1)S(1)}, bf16[4096,128]{1,0:T(8,128)(2,1)}, u32[]{:S(2)}, u32[]{:S(2)}) %collective-permute-start.3) | collective-permute-done | bytes 1048608 | tf_op jit(solution)/shard_map/ppermute | solution.py:47
  134.2 2.3 collective-permute-start.4
  137.2 2.4 constant_dynamic-update-slice_fusion.15
  139.7 9.4 %collective-permute-done.4 = bf16[4096,128]{1,0:T(8,128)(2,1)} collective-permute-done((bf16[4096,128]{1,0:T(8,128)(2,1)}, bf16[4096,128]{1,0:T(8,128)(2,1)}, u32[]{:S(2)}, u32[]{:S(2)}) %collective-permute-start.4) | collective-permute-done | bytes 1048608 | tf_op jit(solution)/shard_map/ppermute | solution.py:47
  149.1 2.2 collective-permute-start.5
  151.3 1.1 constant_dynamic-update-slice_fusion.14
  152.5 1.2 constant_dynamic-update-slice_fusion.13
  153.6 2.3 constant_dynamic-update-slice_fusion.12
  155.9 8.0 %collective-permute-done.5 = bf16[4096,128]{1,0:T(8,128)(2,1)S(1)} collective-permute-done((bf16[4096,128]{1,0:T(8,128)(2,1)}, bf16[4096,128]{1,0:T(8,128)(2,1)S(1)}, u32[]{:S(2)}, u32[]{:S(2)}) %collective-permute-start.5) | collective-permute-done | bytes 1048608 | tf_op jit(solution)/shard_map/ppermute | solution.py:47
  163.9 1.8 collective-permute-start.6
  165.7 2.4 constant_dynamic-update-slice_fusion.11
  168.1 2.3 constant_dynamic-update-slice_fusion.10
  170.4 1.1 constant_dynamic-update-slice_fusion.9
  171.6 6.5 %collective-permute-done.6 = bf16[4096,128]{1,0:T(8,128)(2,1)S(1)} collective-permute-done((bf16[4096,128]{1,0:T(8,128)(2,1)S(1)}, bf16[4096,128]{1,0:T(8,128)(2,1)S(1)}, u32[]{:S(2)}, u32[]{:S(2)}) %collective-permute-start.6) | collective-permute-done | bytes 1048608 | tf_op jit(solution)/shard_map/ppermute | solution.py:47
  178.1 1.1 constant_dynamic-update-slice_fusion.8
  179.2 1.1 constant_dynamic-update-slice_fusion.7
  180.3 1.2 constant_dynamic-update-slice_fusion.6
  181.5 1.1 constant_dynamic-update-slice_fusion.5
  182.6 1.1 constant_dynamic-update-slice_fusion.4
  183.7 2.4 constant_dynamic-update-slice_fusion.3
  186.0 2.3 constant_dynamic-update-slice_fusion.2
  189.5 1.1 constant_dynamic-update-slice_fusion
  190.6 15.3 %fusion = f32[1024,1024]{1,0:T(8,128)S(1)} fusion(bf16[4096,1024]{1,0:T(8,128)(2,1)} %all-gather.5.cloned.1.call-done, bf16[4096,2048]{1,0:T(8,128)(2,1)} %constant_dynamic-update-slice_fusion, s32[]{:T(128)S(6)} %select_n.18, pred[4096]{0:T(1024)(128)(4,1)S(1)} %bitcast.7), kind=kOutput, calls=%fused_computation | convolution fusion | flops 8594128896 | bytes 20975620 | tf_op jit(solution)/shard_map/dot_general | solution.py:33
  205.9 97.2 %all_to_all.5 = f32[4,256,1024]{2,1,0:T(8,128)} all-to-all(f32[4,256,1024]{2,1,0:T(8,128)S(1)} %bitcast.6), channel_id=1, replica_groups=mesh['gx'=4,'gy_0'=4,'gy_1'=2,'gz'=8] {'gx'}, dimensions={0} | all-to-all | bytes 8388608 | tf_op jit(solution)/shard_map/all_to_all | solution.py:28
  303.1 3.7 %reduce_sum.9 = f32[256,1024]{1,0:T(8,128)} reduce(f32[4,256,1024]{2,1,0:T(8,128)} %all_to_all.5, f32[]{:T(128)} %constant.31.clone.1), dimensions={0}, to_apply=%region_0.1 | reduce | flops 786432 | bytes 5242884 | tf_op jit(solution)/shard_map/reduce_sum | solution.py:29
  (15 shorter events, 3.6 us)
Async XLA Ops:
  6.5 172.6 %copy-start = (bf16[4096,128]{1,0:T(8,128)(2,1)S(1)}, bf16[4096,128]{1,0:T(8,128)(2,1)}, u32[]{:S(2)}) copy-start(bf16[4096,128]{1,0:T(8,128)(2,1)} %param.3) | copy-start | bytes 3145732
  6.5 70.6 %all-gather.3.cloned.1.call-start = ((), (), s32[]{:S(2)}) async-start(), calls=%async_computation.1 | async-start | bytes 3145728 | tf_op jit(solution)/shard_map/all_gather | solution.py:16
  7.3 183.3 %all-gather.5.cloned.1.call-start = ((), (), s32[]{:S(2)}) async-start(), calls=%async_computation.2 | async-start | bytes 10485760 | tf_op jit(solution)/shard_map/all_gather | solution.py:16
  77.2 12.7 %collective-permute-start = (bf16[4096,128]{1,0:T(8,128)(2,1)}, bf16[4096,128]{1,0:T(8,128)(2,1)S(1)}, u32[]{:S(2)}, u32[]{:S(2)}) collective-permute-start(bf16[4096,128]{1,0:T(8,128)(2,1)} %param.3), channel_id=1, source_target_pairs={{0,7},{1,0},{2,1},{3,2},{4,3},{5,4},{6,5},{7,6},{8,15},{9,8},{10,9... | collective-permute-start | bytes 3145736 | tf_op jit(solution)/shard_map/ppermute | solution.py:47
  89.8 14.1 %collective-permute-start.1 = (bf16[4096,128]{1,0:T(8,128)(2,1)S(1)}, bf16[4096,128]{1,0:T(8,128)(2,1)S(1)}, u32[]{:S(2)}, u32[]{:S(2)}) collective-permute-start(bf16[4096,128]{1,0:T(8,128)(2,1)S(1)} %collective-permute-done), channel_id=1, source_target_pairs={{0,7},{1,0},{2,1},{3,2},{4,3},{5,4},{6,5},{7,6},{8,15},{9,8},{10,9... | collective-permute-start | bytes 3145736 | tf_op jit(solution)/shard_map/ppermute | solution.py:47
  103.9 14.6 %collective-permute-start.2 = (bf16[4096,128]{1,0:T(8,128)(2,1)S(1)}, bf16[4096,128]{1,0:T(8,128)(2,1)S(1)}, u32[]{:S(2)}, u32[]{:S(2)}) collective-permute-start(bf16[4096,128]{1,0:T(8,128)(2,1)S(1)} %collective-permute-done.1), channel_id=1, source_target_pairs={{0,7},{1,0},{2,1},{3,2},{4,3},{5,4},{6,5},{7,6},{8,15},{9,8},{10,9... | collective-permute-start | bytes 3145736 | tf_op jit(solution)/shard_map/ppermute | solution.py:47
  118.6 1.0 copy-start.1
  119.5 14.6 %collective-permute-start.3 = (bf16[4096,128]{1,0:T(8,128)(2,1)S(1)}, bf16[4096,128]{1,0:T(8,128)(2,1)}, u32[]{:S(2)}, u32[]{:S(2)}) collective-permute-start(bf16[4096,128]{1,0:T(8,128)(2,1)S(1)} %collective-permute-done.2), channel_id=1, source_target_pairs={{0,7},{1,0},{2,1},{3,2},{4,3},{5,4},{6,5},{7,6},{8,15},{9,8},{10,9... | collective-permute-start | bytes 3145736 | tf_op jit(solution)/shard_map/ppermute | solution.py:47
  134.2 14.9 %collective-permute-start.4 = (bf16[4096,128]{1,0:T(8,128)(2,1)}, bf16[4096,128]{1,0:T(8,128)(2,1)}, u32[]{:S(2)}, u32[]{:S(2)}) collective-permute-start(bf16[4096,128]{1,0:T(8,128)(2,1)} %collective-permute-done.3), channel_id=1, source_target_pairs={{0,7},{1,0},{2,1},{3,2},{4,3},{5,4},{6,5},{7,6},{8,15},{9,8},{10,9... | collective-permute-start | bytes 3145736 | tf_op jit(solution)/shard_map/ppermute | solution.py:47
  137.2 45.4 %copy-start.2 = (bf16[4096,128]{1,0:T(8,128)(2,1)S(1)}, bf16[4096,128]{1,0:T(8,128)(2,1)}, u32[]{:S(2)}) copy-start(bf16[4096,128]{1,0:T(8,128)(2,1)} %copy-done.1) | copy-start | bytes 3145732
  149.1 14.8 %collective-permute-start.5 = (bf16[4096,128]{1,0:T(8,128)(2,1)}, bf16[4096,128]{1,0:T(8,128)(2,1)S(1)}, u32[]{:S(2)}, u32[]{:S(2)}) collective-permute-start(bf16[4096,128]{1,0:T(8,128)(2,1)} %collective-permute-done.4), channel_id=1, source_target_pairs={{0,7},{1,0},{2,1},{3,2},{4,3},{5,4},{6,5},{7,6},{8,15},{9,8},{10,9... | collective-permute-start | bytes 3145736 | tf_op jit(solution)/shard_map/ppermute | solution.py:47
  163.9 14.1 %collective-permute-start.6 = (bf16[4096,128]{1,0:T(8,128)(2,1)S(1)}, bf16[4096,128]{1,0:T(8,128)(2,1)S(1)}, u32[]{:S(2)}, u32[]{:S(2)}) collective-permute-start(bf16[4096,128]{1,0:T(8,128)(2,1)S(1)} %collective-permute-done.5), channel_id=1, source_target_pairs={{0,7},{1,0},{2,1},{3,2},{4,3},{5,4},{6,5},{7,6},{8,15},{9,8},{10,9... | collective-permute-start | bytes 3145736 | tf_op jit(solution)/shard_map/ppermute | solution.py:47
Sparse Core Ops, SparseCore 0:
  9.1 67.9 all-gather.2
  78.9 85.4 all-gather.4
